TPU v7x, 32 devices: a whole 2x2x4 slice. The times are simulated.
32 devices in a mesh: groups: 2 (over x), tp: 8 (over z, y), blk: 2 (over core).
Axes of the slice: x: 2, y: 2, z: 4, core: 2. Of those that a mesh axis runs over, the one named last changes fastest.
Arguments:
- tokens: bfloat16 [4096, 7168], P(('groups', 'tp')), parts along dimension 0, may hold values from -6 to 6
- gate_weight: bfloat16 [7168, 2048], P('tp', 'blk'), may hold values from -0.0625 to 0.0625
- up_weight: bfloat16 [7168, 2048], P('tp', 'blk'), may hold values from -0.0625 to 0.0625
- down_weight: bfloat16 [2048, 7168], P('blk', 'tp'), may hold values from -0.125 to 0.125
Outputs:
- mixed: bfloat16 [4096, 7168], P(('groups', 'blk'), 'tp'), parts along dimension 0
There are 2 independent parts, one for each index of `groups`. A program takes and returns all parts, laid end to end along the dimension named above; an argument that names none is the same for every part. Nothing has to cross between parts.
All inputs are finite; a program needn't handle non-finite values.
Results may differ from a plain program's by a relative error of at most 0.005.
Values may be sent and summed in bfloat16 or wider, within the bound.
A program may use at most 128 MiB of HBM per device.

v0:
```python
import jax
import jax.numpy as jnp
from jax import lax
from jax.sharding import PartitionSpec as P


def local(tokens, gate_weight, up_weight, down_weight):
    gate_part = jnp.dot(
        tokens,
        lax.all_gather(gate_weight, "tp", axis=0, tiled=True),
        preferred_element_type=jnp.float32,
    )
    up_part = jnp.dot(
        tokens,
        lax.all_gather(up_weight, "tp", axis=0, tiled=True),
        preferred_element_type=jnp.float32,
    )
    hidden = (jax.nn.silu(gate_part) * up_part).astype(jnp.bfloat16)
    gathered = lax.all_gather(hidden, "tp", axis=0, tiled=True)
    own_units = lax.all_to_all(gathered, "blk", split_axis=0, concat_axis=1, tiled=True)
    down_full = lax.all_gather(down_weight, "blk", axis=0, tiled=True)
    result = jnp.dot(own_units, down_full, preferred_element_type=jnp.float32)
    return result.astype(jnp.bfloat16)


def solution(mesh):
    return jax.shard_map(
        local,
        mesh=mesh,
        in_specs=(P(("groups", "tp"), None), P("tp", "blk"), P("tp", "blk"), P("blk", "tp")),
        out_specs=P(("groups", "blk"), "tp"),
        check_vma=False,
    )
```

profile of v0, /device:TPU:28, one launch (start us, length us, event | category | flops | bytes accessed | tf_op | source)
XLA Modules:
  0.0 528.2 jit_solution(12238021908030570183)
XLA Ops:
  6.5 0.0 all-gather.5.cloned.1.call-start
  6.5 0.7 all-gather.5.cloned.1.call-update
  7.3 0.0 all-gather.7.cloned.1.call-start
  7.3 0.7 all-gather.7.cloned.1.call-update
  8.0 0.0 all-gather.9.cloned.1.call-start
  8.1 201.2 %all-gather.5.cloned.1.call-done = bf16[7168,1024]{1,0:T(8,128)(2,1)} async-done(((bf16[896,1024]{1,0:T(8,128)(2,1)}), bf16[7168,1024]{1,0:T(8,128)(2,1)}) %all-gather.5.cloned.1.call-update) | async-done | bytes 14680080 | tf_op jit(solution)/shard_map/all_gather | solution.py:10
  209.3 8.4 %fusion.1 = f32[256,1024]{1,0:T(8,128)S(1)} fusion(bf16[256,7168]{1,0:T(8,128)(2,1)} %param.4, bf16[7168,1024]{1,0:T(8,128)(2,1)} %all-gather.5.cloned.1.call-done), kind=kOutput, calls=%fused_computation.3 | convolution fusion | flops 3758096384 | bytes 19398656 | tf_op jit(solution)/shard_map/dot_general | solution.py:8
  217.7 193.6 %all-gather.7.cloned.1.call-done = bf16[7168,1024]{1,0:T(8,128)(2,1)} async-done(((bf16[896,1024]{1,0:T(8,128)(2,1)}), bf16[7168,1024]{1,0:T(8,128)(2,1)}) %all-gather.7.cloned.1.call-update) | async-done | bytes 14680080 | tf_op jit(solution)/shard_map/all_gather | solution.py:15
  411.4 11.1 %fusion = bf16[256,1024]{1,0:T(8,128)(2,1)} fusion(bf16[256,7168]{1,0:T(8,128)(2,1)} %param.4, bf16[7168,1024]{1,0:T(8,128)(2,1)} %all-gather.7.cloned.1.call-done, f32[256,1024]{1,0:T(8,128)S(1)} %fusion.1), kind=kOutput, calls=%fused_computation.2 | convolution fusion | flops 3759669248 | bytes 19922944 | tf_op jit(solution)/shard_map/dot_general | solution.py:13
  422.5 0.0 all-gather.9.cloned.1.call-update
  422.5 0.0 all-gather.11.cloned.1.call-start
  422.6 0.5 all-gather.11.cloned.1.call-update
  423.1 71.0 %all-gather.9.cloned.1.call-done = bf16[2048,1024]{1,0:T(8,128)(2,1)} async-done(((bf16[256,1024]{1,0:T(8,128)(2,1)}), bf16[2048,1024]{1,0:T(8,128)(2,1)}) %all-gather.9.cloned.1.call-update) | async-done | bytes 4194320 | tf_op jit(solution)/shard_map/all_gather | solution.py:19
  494.1 6.2 %copy.5 = bf16[2,1024,1024]{1,2,0:T(8,128)(2,1)} copy(bf16[2,1024,1024]{2,1,0:T(8,128)(2,1)} %bitcast.10) | data formatting | bytes 8388608 | tf_op jit(solution)/shard_map/all_to_all | solution.py:20
  500.3 5.8 %all-to-all-start = ((bf16[2,1024,1024]{1,2,0:T(8,128)(2,1)}), bf16[2,1024,1024]{1,2,0:T(8,128)(2,1)}, u32[]{:S(2)}, u32[]{:S(2)}) async-start(bf16[2,1024,1024]{1,2,0:T(8,128)(2,1)} %copy.5), calls=%async_computation | async-start | bytes 8388608 | tf_op jit(solution)/shard_map/all_to_all | solution.py:20
  506.2 5.7 %all-gather.11.cloned.1.call-done = bf16[2048,896]{1,0:T(8,128)(2,1)} async-done(((bf16[1024,896]{1,0:T(8,128)(2,1)}), bf16[2048,896]{1,0:T(8,128)(2,1)}) %all-gather.11.cloned.1.call-update) | async-done | bytes 3670032 | tf_op jit(solution)/shard_map/all_gather | solution.py:21
  511.9 0.7 all-to-all-done
  512.6 9.1 %convolution_convert_fusion = bf16[1024,896]{1,0:T(8,128)(2,1)} fusion(bf16[1024,2048]{0,1:T(8,128)(2,1)} %bitcast.2, bf16[2048,896]{1,0:T(8,128)(2,1)} %all-gather.11.cloned.1.call-done), kind=kOutput, calls=%fused_computation | convolution fusion | flops 3759013888 | bytes 9699328 | tf_op jit(solution)/shard_map/dot_general | solution.py:22
Async XLA Ops:
  6.5 202.8 %all-gather.5.cloned.1.call-start = ((), (), s32[]{:S(2)}) async-start(), calls=%async_computation.1 | async-start | bytes 16515072 | tf_op jit(solution)/shard_map/all_gather | solution.py:10
  7.3 404.1 %all-gather.7.cloned.1.call-start = ((), (), s32[]{:S(2)}) async-start(), calls=%async_computation.2 | async-start | bytes 16515072 | tf_op jit(solution)/shard_map/all_gather | solution.py:15
  8.0 486.1 %all-gather.9.cloned.1.call-start = ((), (), s32[]{:S(2)}) async-start(), calls=%async_computation.3 | async-start | bytes 4718592 | tf_op jit(solution)/shard_map/all_gather | solution.py:19
  422.5 89.4 %all-gather.11.cloned.1.call-start = ((), (), s32[]{:S(2)}) async-start(), calls=%async_computation.4 | async-start | bytes 5505024 | tf_op jit(solution)/shard_map/all_gather | solution.py:21
  500.3 12.2 %all-to-all-start = ((bf16[2,1024,1024]{1,2,0:T(8,128)(2,1)}), bf16[2,1024,1024]{1,2,0:T(8,128)(2,1)}, u32[]{:S(2)}, u32[]{:S(2)}) async-start(bf16[2,1024,1024]{1,2,0:T(8,128)(2,1)} %copy.5), calls=%async_computation | async-start | bytes 8388608 | tf_op jit(solution)/shard_map/all_to_all | solution.py:20
Sparse Core Ops, SparseCore 0:
  9.5 199.7 all-gather.4
  211.5 199.8 all-gather.6
  422.6 71.4 all-gather.8
  495.5 16.3 all-gather.10
where the time goes:
time: 531 us; the launch traced here: 528 us
  waiting for transfers between devices  474 us (89%)
  matrix products  28.7 us (5%)
  between operations  13.1 us (2%)
  local copies, waits for them, and re-layouts  6.23 us (1%)
  starting transfers between devices  5.96 us (1%)
    all_gather x1, waiting for transfers between devices, local(): lax.all_gather(gate_weight, 'tp', axis=0, tiled=True)  201 us
    all_gather x1, waiting for transfers between devices, local(): lax.all_gather(up_weight, 'tp', axis=0, tiled=True)  194 us
    all_gather x1, waiting for transfers between devices, local(): gathered = lax.all_gather(hidden, 'tp', axis=0, tiled=True)  71 us
    dot_general x1, matrix products, local(): jnp.dot(tokens, lax.all_gather(up_weight, 'tp', axis=0, tiled=True), pref...  11.1 us
  transfers between devices with their start and end apart: 5, of which 5 were waited for; matrix products, arithmetic and copies ran while one was open for 3% of the time, Pallas kernels for 0%

commit v1 on v0

v1 whole, which is shorter than its diff:
```python
import functools

import jax
import jax.numpy as jnp
from jax import lax
from jax.experimental import pallas as pl
from jax.experimental.pallas import tpu as pltpu
from jax.sharding import PartitionSpec as P

MESH = pl.DeviceIdType.MESH
ANY = pl.BlockSpec(memory_space=pl.ANY)


def flip1(i):
    return i + 1 - 2 * (i % 2)


def greet(devices):
    barrier = pltpu.get_barrier_semaphore()
    for device in devices:
        pl.semaphore_signal(barrier, inc=1, device_id=device, device_id_type=MESH)
    pl.semaphore_wait(barrier, len(devices))


def exchange(
    G, n, B,
    tok, gate, up, down, T, W, D,
    v_tok, v_w, v_down,
    lsem, tok_send, tok_recv, core_send, core_recv,
    w_send, w_recv, x_send, x_recv, d_send, d_recv,
):
    g, t, b = lax.axis_index("groups"), lax.axis_index("tp"), lax.axis_index("blk")
    h = n // B
    a, j = t // h, t % h
    other = (g, t, 1 - b)
    width = tok.shape[1] // B
    depth, units = gate.shape[0], gate.shape[1] // h
    part = depth // G
    mine = pl.ds(pl.multiple_of(b * width, 128), width)

    greet(
        [(g, (t + d) % n, b) for d in range(1, n)]
        + [((g + e) % G, t, b) for e in range(1, G)]
        + [other]
    )

    def remote(src, dst, send, recv, device):
        return pltpu.make_async_remote_copy(
            src_ref=src, dst_ref=dst, send_sem=send, recv_sem=recv,
            device_id=device, device_id_type=MESH,
        )

    def local(src, dst, sem):
        return pltpu.make_async_copy(src, dst, sem)

    def token_block(slot):
        return T.at[slot, :, mine]

    own_columns = pl.ds(pl.multiple_of(j * units, 128), units)
    loads = [
        local(tok, v_tok, lsem.at[0]),
        local(gate.at[:, own_columns], v_w.at[:, pl.ds(0, units)], lsem.at[1]),
        local(up.at[:, own_columns], v_w.at[:, pl.ds(units, units)], lsem.at[2]),
        local(down, v_down, lsem.at[3]),
    ]
    for load in loads:
        load.start()

    square = h == 4
    if square:
        def flip2(i):
            return i + 2 - 4 * (i // 2)

        near = [flip1(j), flip2(j)]
        sources = near + [flip1(flip2(j))]
        direct = 2
    else:
        near = [(j + d) % h for d in range(1, h)]
        sources = [(j - d + h) % h for d in range(1, h)]
        direct = h - 1
    pending = []
    for k in range(direct):
        c = remote(tok.at[:, mine], token_block(j), tok_send.at[k], tok_recv.at[k], (g, a * h + near[k], b))
        c.start()
        pending.append(c)

    rows = pl.ds(pl.multiple_of(g * part, 16), part)

    order = [n // 2] + [d for k in range(1, n // 2) for d in (n // 2 - k, n // 2 + k)]

    def weight_copy(d, k):
        src = (gate, up)[k]
        dest = (t + d) % n
        cols = pl.ds(pl.multiple_of((dest % h) * units, 128), units)
        return remote(
            src.at[rows, cols], W.at[t, rows, pl.ds(k * units, units)],
            w_send.at[d, k], w_recv.at[d, k], (g, dest, b),
        )

    for d in order:
        for k in range(2):
            c = weight_copy(d, k)
            c.start()
            pending.append(c)

    c = remote(down, D.at[b], d_send, d_recv, other)
    c.start()
    pending.append(c)

    for load in loads:
        load.wait()
    stores = [
        local(v_tok, T.at[j], lsem.at[0]),
        local(v_w, W.at[t], lsem.at[1]),
        local(v_down, D.at[b], lsem.at[3]),
    ]
    for store in stores:
        store.start()

    def to_other(k):
        block = token_block(sources[k])
        c = remote(block, block, core_send.at[k], core_recv.at[k], other)
        c.start()
        pending.append(c)

    def arrived(k):
        block = token_block(sources[k])
        remote(block, block, tok_send.at[k], tok_recv.at[k], other).wait_recv()

    if square:
        arrived(0)
        arrived(1)
        passed = j + 1 - 2 * (j % 2) + b * (flip2(j) - flip1(j))
        target = flip2(j) + b * (flip1(j) - flip2(j))
        block = token_block(passed)
        c = remote(block, block, tok_send.at[2], tok_recv.at[2], (g, a * h + target, b))
        c.start()
        pending.append(c)
        to_other(0)
        to_other(1)
    else:
        for k in range(h - 1):
            arrived(k)
            to_other(k)

    for d in order:
        source = (t - d + n) % n
        for k in range(2):
            block = W.at[source, rows, pl.ds(k * units, units)]
            remote(block, block, w_send.at[d, k], w_recv.at[d, k], other).wait_recv()
            for e in range(1, G):
                c = remote(block, block, x_send.at[e, d, k], x_recv.at[e, d, k], ((g + e) % G, t, b))
                c.start()
                pending.append(c)
    if square:
        arrived(2)
        to_other(2)

    theirs = pl.ds(pl.multiple_of((1 - b) * width, 128), width)
    for k in range(h - 1):
        block = T.at[sources[k], :, theirs]
        remote(block, block, core_send.at[k], core_recv.at[k], other).wait_recv()
    for d in order:
        source = (t - d + n) % n
        for e in range(1, G):
            their_rows = pl.ds(pl.multiple_of(((g - e + G) % G) * part, 16), part)
            for k in range(2):
                block = W.at[source, their_rows, pl.ds(k * units, units)]
                remote(block, block, x_send.at[e, d, k], x_recv.at[e, d, k], other).wait_recv()
    remote(D.at[1 - b], D.at[1 - b], d_send, d_recv, other).wait_recv()
    for c in pending:
        c.wait_send()
    for store in stores:
        store.wait()


def spread(n, B, hid, H, v_hid, lsem, send, recv, f_send, f_recv):
    g, t, b = lax.axis_index("groups"), lax.axis_index("tp"), lax.axis_index("blk")
    h = n // B
    a = t // h
    half, pairs = h // 2, n // 2
    p, y = t // 2, t % 2
    units = hid.shape[1]
    other = (g, t, 1 - b)
    across = (g, flip1(t), b)

    greet(
        [(g, (2 * ((p + d) % pairs) + y), c) for d in range(1, pairs) for c in range(B)]
        + [other, across]
    )

    def remote(src, dst, s, r, device):
        return pltpu.make_async_remote_copy(
            src_ref=src, dst_ref=dst, send_sem=s, recv_sem=r,
            device_id=device, device_id_type=MESH,
        )

    def columns(k, yy, c):
        return pl.ds(pl.multiple_of((c * h + 2 * k + yy) * units, 128), units)

    own = p % half
    place = H.at[:, columns(own, y, b)]
    load = pltpu.make_async_copy(hid, v_hid, lsem)
    load.start()
    copies = []
    for d in sorted(range(1, pairs), key=lambda d: -min(d, pairs - d)):
        c = remote(hid, place, send.at[d], recv.at[own, b], (g, 2 * ((p + d) % pairs) + y, a))
        c.start()
        copies.append(c)
    load.wait()

    @pl.when(a == b)
    def _():
        pltpu.make_async_copy(v_hid, place, recv.at[own, b]).start()

    @pl.when(a != b)
    def _():
        c = remote(hid, place, send.at[0], recv.at[own, b], other)
        c.start()
        c.wait_send()

    for k in range(half):
        for c in range(B):
            block = H.at[:, columns(k, y, c)]
            remote(block, block, send.at[0], recv.at[k, c], other).wait_recv()
            f = remote(block, block, f_send.at[k, c], f_recv.at[k, c], across)
            f.start()
            copies.append(f)
    for k in range(half):
        for c in range(B):
            block = H.at[:, columns(k, 1 - y, c)]
            remote(block, block, f_send.at[k, c], f_recv.at[k, c], across).wait_recv()
    for c in copies:
        c.wait_send()


def local(G, n, B, tokens, gate_weight, up_weight, down_weight):
    h = n // B
    R, K = tokens.shape
    depth, wide = gate_weight.shape
    units = wide // h
    dtype = tokens.dtype
    DMA = pltpu.SemaphoreType.DMA
    T, W, D = pl.pallas_call(
        functools.partial(exchange, G, n, B),
        out_shape=[
            jax.ShapeDtypeStruct((h, R, K), dtype),
            jax.ShapeDtypeStruct((n, depth, 2 * units), dtype),
            jax.ShapeDtypeStruct((B,) + down_weight.shape, dtype),
        ],
        in_specs=[ANY] * 4,
        out_specs=[ANY] * 3,
        scratch_shapes=[
            pltpu.VMEM((R, K), dtype),
            pltpu.VMEM((depth, 2 * units), dtype),
            pltpu.VMEM(down_weight.shape, dtype),
            DMA((4,)),
            DMA((h,)), DMA((h,)), DMA((h,)), DMA((h,)),
            DMA((n, 2)), DMA((n, 2)),
            DMA((G, n, 2)), DMA((G, n, 2)),
            DMA, DMA,
        ],
        compiler_params=pltpu.CompilerParams(collective_id=0, has_side_effects=True),
        name="exchange",
    )(tokens, gate_weight, up_weight, down_weight)
    both = jnp.dot(
        T.reshape(h * R, K), W.reshape(n * depth, 2 * units),
        preferred_element_type=jnp.float32,
    )
    hidden = (jax.nn.silu(both[:, :units]) * both[:, units:]).astype(dtype)
    half = h // 2
    H = pl.pallas_call(
        functools.partial(spread, n, B),
        out_shape=jax.ShapeDtypeStruct((h * R, B * wide), dtype),
        in_specs=[ANY],
        out_specs=ANY,
        scratch_shapes=[
            pltpu.VMEM((h * R, units), dtype),
            DMA,
            DMA((n // 2,)), DMA((half, B)), DMA((half, B)), DMA((half, B)),
        ],
        compiler_params=pltpu.CompilerParams(collective_id=1, has_side_effects=True),
        name="spread",
    )(hidden)
    result = jnp.dot(H, D.reshape(B * down_weight.shape[0], -1), preferred_element_type=jnp.float32)
    return result.astype(dtype)


def solution(mesh):
    shape = dict(mesh.shape)
    return jax.shard_map(
        functools.partial(local, shape["groups"], shape["tp"], shape["blk"]),
        mesh=mesh,
        in_specs=(P(("groups", "tp"), None), P("tp", "blk"), P("tp", "blk"), P("blk", "tp")),
        out_specs=P(("groups", "blk"), "tp"),
        check_vma=False,
    )
```

time: 531 us -> 253 us (0.48)
  waiting for transfers between devices: 474 us -> 0 us
  Pallas kernels: 0 us -> 230 us
  between operations: 13.1 us -> 0.03 us
  matrix products: 28.7 us -> 21.8 us
  local copies, waits for them, and re-layouts: 6.23 us -> 0 us
  starting transfers between devices: 5.96 us -> 0 us
    all_gather x4 -> x0, waiting for transfers between devices: 472 us -> none  [the longest x1 201 us: local(): lax.all_gather(gate_weight, 'tp', axis=0, tiled=True)]
    pallas_call x0 -> x2, Pallas kernels: none -> 230 us  [the longest x1 134 us: local(): pl.pallas_call(functools.partial(exchange, G, n, B), out_shape=[jax.Shape...]
    dot_general x3 -> x2, matrix products: 28.7 us -> 21.8 us  [the longest x1 12.8 us: local(): jnp.dot(T.reshape(h * R, K), W.reshape(n * depth, 2 * units), preferred_e...]
    all_to_all x1 -> x0, local copies, waits for them, and re-layouts: 6.23 us -> none  [local(): lax.all_to_all(gathered, 'blk', split_axis=0, concat_axis=1, tiled=True)]
    all_to_all x1 -> x0, starting transfers between devices: 5.84 us -> none  [local(): lax.all_to_all(gathered, 'blk', split_axis=0, concat_axis=1, tiled=True)]
  transfers between devices with their start and end apart: 5 -> 0, of which waited for: 5 -> 0; matrix products, arithmetic and copies ran while one was open for 3% -> 0% of each run, Pallas kernels for 0% -> 0%
where the time goes in v1:
time: 253 us
  Pallas kernels  230 us (91%)
  matrix products  21.8 us (9%)
    pallas_call x1, Pallas kernels, local(): pl.pallas_call(functools.partial(exchange, G, n, B), out_shape=[jax.Shape...  134 us
    pallas_call x1, Pallas kernels, local(): pl.pallas_call(functools.partial(spread, n, B), out_shape=jax.ShapeDtypeS...  96.4 us
    dot_general x1, matrix products, local(): jnp.dot(T.reshape(h * R, K), W.reshape(n * depth, 2 * units), preferred_e...  12.8 us
    dot_general x1, matrix products, local(): jnp.dot(H, D.reshape(B * down_weight.shape[0], -1), preferred_element_typ...  9.03 us

profile of v1, /device:TPU:28, one launch (start us, length us, event | category | flops | bytes accessed | tf_op | source)
XLA Modules:
  0.0 252.9 jit_solution(53951745794285291)
XLA Ops:
  0.0 133.5 %exchange.1 = (bf16[4,256,7168]{2,1,0:T(8,128)(2,1)}, bf16[8,896,512]{2,1,0:T(8,128)(2,1)}, bf16[2,1024,896]{2,1,0:T(8,128)(2,1)}) custom-call(bf16[256,7168]{1,0:T(8,128)(2,1)} %tok.1, bf16[896,1024]{1,0:T(8,128)(2,1)} %gate.1, bf16[896,1024]{1,0:T(8,128)(2,1)} %up.1, bf16[1024,896]{1,0:T(8,128)(2,1)} %down.1), custom_call_target="tpu_custom_call" | custom-call | tf_op jit(solution)/shard_map/exchange/pallas_call | solution.py:244
  133.6 12.8 %fusion.1 = f32[1024,512]{1,0:T(8,128)S(1)} fusion(bf16[1024,7168]{1,0:T(8,128)(2,1)} %bitcast.7, bf16[7168,512]{1,0:T(8,128)(2,1)} %bitcast.8), kind=kOutput, calls=%fused_computation.3 | convolution fusion | flops 7516192768 | bytes 24117248 | tf_op jit(solution)/shard_map/dot_general | solution.py:266
  146.3 1.1 fusion.hid
  147.4 96.4 %spread.1 = bf16[1024,2048]{1,0:T(8,128)(2,1)} custom-call(bf16[1024,256]{1,0:T(8,128)(2,1)} %fusion.hid), custom_call_target="tpu_custom_call" | custom-call | tf_op jit(solution)/shard_map/spread/pallas_call | solution.py:272
  243.9 9.0 %convolution_convert_fusion = bf16[1024,896]{1,0:T(8,128)(2,1)} fusion(bf16[1024,2048]{1,0:T(8,128)(2,1)} %spread.1, bf16[2048,896]{1,0:T(8,128)(2,1)} %bitcast.9), kind=kOutput, calls=%fused_computation | convolution fusion | flops 3759013888 | bytes 9699328 | tf_op jit(solution)/shard_map/dot_general | solution.py:285

commit v2 on v0

v2 whole, which is shorter than its diff:
```python
import functools

import jax
import jax.numpy as jnp
from jax import lax
from jax.experimental import pallas as pl
from jax.experimental.pallas import tpu as pltpu
from jax.sharding import PartitionSpec as P

MESH = pl.DeviceIdType.MESH
ANY = pl.BlockSpec(memory_space=pl.ANY)


def flip1(i):
    return i + 1 - 2 * (i % 2)


def greet(devices):
    barrier = pltpu.get_barrier_semaphore()
    for device in devices:
        pl.semaphore_signal(barrier, inc=1, device_id=device, device_id_type=MESH)
    pl.semaphore_wait(barrier, len(devices))


def flip2(i):
    return i + 2 - 4 * ((i // 2) % 2)


def layer(
    G, n, B,
    tok, gate, up, down, out,
    T, W, D, both, mine_h, H, total,
    lsem, tok_send, tok_recv, core_send, core_recv,
    w_send, w_recv, x_send, x_recv, d_send, d_recv,
    h_send, h_recv, f_send, f_recv,
):
    g, t, b = lax.axis_index("groups"), lax.axis_index("tp"), lax.axis_index("blk")
    h = n // B
    a, j = t // h, t % h
    half, pairs = h // 2, n // 2
    p, y = t // 2, t % 2
    other = (g, t, 1 - b)
    across = (g, flip1(t), a * 0 + b)
    R, K = tok.shape
    width = K // B
    depth, units = gate.shape[0], gate.shape[1] // h
    part = depth // G
    mine = pl.ds(pl.multiple_of(b * width, 128), width)
    theirs = pl.ds(pl.multiple_of((1 - b) * width, 128), width)
    square = h == 4

    greet(
        [(g, (t + d) % n, b) for d in range(1, n)]
        + [(g, 2 * ((p + d) % pairs) + y, 1 - b) for d in range(1, pairs)]
        + [((g + e) % G, t, b) for e in range(1, G)]
        + [other]
    )

    def remote(src, dst, send, recv, device):
        return pltpu.make_async_remote_copy(
            src_ref=src, dst_ref=dst, send_sem=send, recv_sem=recv,
            device_id=device, device_id_type=MESH,
        )

    pending = []

    def push(*copy):
        c = remote(*copy)
        c.start()
        pending.append(c)

    def local(src, dst, sem):
        return pltpu.make_async_copy(src, dst, sem)

    def rows_of(i, s):
        if square:
            i = flip1(i) if s % 2 else i
            return flip2(i) if s // 2 else i
        return (i + h - s) % h

    def token_block(s):
        return T.at[rows_of(j, s), :, mine]

    def w_block(source, first, size, k):
        start = pl.multiple_of(source * depth + first, 16)
        return W.at[pl.ds(start, size), pl.ds(k * units, units)]

    own_columns = pl.ds(pl.multiple_of(j * units, 128), units)
    loads = [
        local(gate.at[:, own_columns], w_block(t, 0, depth, 0), lsem.at[0]),
        local(up.at[:, own_columns], w_block(t, 0, depth, 1), lsem.at[1]),
        local(tok, T.at[j], lsem.at[2]),
        local(down, D.at[b], lsem.at[3]),
    ]

    first = g * part
    rows = pl.ds(pl.multiple_of(first, 16), part)
    order = [n // 2] + [d for k in range(1, n // 2) for d in (n // 2 - k, n // 2 + k)]
    for d in order:
        dest = (t + d) % n
        cols = pl.ds(pl.multiple_of((dest % h) * units, 128), units)
        for k in range(2):
            push(
                (gate, up)[k].at[rows, cols], w_block(t, first, part, k),
                w_send.at[d, k], w_recv.at[d, k], (g, dest, b),
            )

    for s in (2, 1) if square else range(1, h):
        dest = rows_of(j, s) if square else (j + s) % h
        push(tok.at[:, mine], T.at[j, :, mine], tok_send.at[s], tok_recv.at[s], (g, a * h + dest, b))
    push(down, D.at[b], d_send, d_recv, other)
    for load in loads:
        load.start()

    for d in order:
        source = (t + n - d) % n
        for k in range(2):
            block = w_block(source, first, part, k)
            remote(block, block, w_send.at[d, k], w_recv.at[d, k], other).wait_recv()
            for e in range(1, G):
                push(block, block, x_send.at[e, d, k], x_recv.at[e, d, k], ((g + e) % G, t, b))
    for load in loads:
        load.wait()
    remote(D.at[1 - b], D.at[1 - b], d_send, d_recv, other).wait_recv()
    total[...] = jnp.zeros_like(total)

    def tokens_arrive(s):
        block = token_block(s)
        remote(block, block, tok_send.at[s], tok_recv.at[s], other).wait_recv()
        if square and s < 3:
            @pl.when(b == s - 1)
            def _():
                target = flip2(j) if s == 1 else flip1(j)
                remote(block, block, tok_send.at[3], tok_recv.at[3], (g, a * h + target, b)).start()

        push(block, block, core_send.at[s], core_recv.at[s], other)

    def compute(s):
        slot = rows_of(j, s)
        if s > 0:
            block = T.at[slot, :, theirs]
            remote(block, block, core_send.at[s], core_recv.at[s], other).wait_recv()
        tiles = 4 if K % 512 == 0 else 1
        tile = K // tiles
        both[...] = jnp.zeros_like(both)

        def body(i, carry):
            k = pl.ds(pl.multiple_of(i * tile, 128), tile)
            both[...] += jnp.dot(T[slot, :, k], W[k, :], preferred_element_type=jnp.float32)
            return carry

        lax.fori_loop(0, tiles, body, 0)
        hidden = (jax.nn.silu(both[:, :units]) * both[:, units:]).astype(out.dtype)
        mine_h[s] = hidden

        @pl.when(a == b)
        def _():
            H[s, j, b] = hidden

        for d in sorted(range(1, pairs), key=lambda d: -min(d, pairs - d)):
            push(
                mine_h.at[s], H.at[s, j, b], h_send.at[s, d], h_recv.at[s, j // 2, b],
                (g, 2 * ((p + d) % pairs) + y, a),
            )

        @pl.when(a != b)
        def _():
            remote(mine_h.at[s], H.at[s, j, b], h_send.at[s, 0], h_recv.at[s, j // 2, b], other).start()

    def pass_on(s):
        for k in range(half):
            for c in range(B):
                block = H.at[s, 2 * k + y, c]

                @pl.when(jnp.logical_not((a == b) & (j // 2 == k) & (c == b)))
                def _():
                    remote(block, block, h_send.at[s, 0], h_recv.at[s, k, c], other).wait_recv()

                push(block, block, f_send.at[s, k, c], f_recv.at[s, k, c], across)

    def lower(s):
        for k in range(half):
            for c in range(B):
                block = H.at[s, 2 * k + 1 - y, c]
                remote(block, block, f_send.at[s, k, c], f_recv.at[s, k, c], across).wait_recv()

        def body(i, carry):
            r = rows_of(i, s)
            term = total[r]
            for c in range(B):
                term += jnp.dot(
                    H[s, i, c], D[c, pl.ds(pl.multiple_of(i * units, 128), units), :],
                    preferred_element_type=jnp.float32,
                )
            total[r] = term
            return carry

        lax.fori_loop(0, h, body, 0)

    for d in order:
        source = (t + n - d) % n
        for e in range(1, G):
            for k in range(2):
                block = w_block(source, ((g + G - e) % G) * part, part, k)
                remote(block, block, x_send.at[e, d, k], x_recv.at[e, d, k], other).wait_recv()

    compute(0)
    for s in range(1, h):
        tokens_arrive(s)
        compute(s)
        pass_on(s - 1)
        if s >= 2:
            lower(s - 2)
    pass_on(h - 1)
    lower(h - 2)
    lower(h - 1)
    for r in range(h):
        out[pl.ds(r * R, R), :] = total[r].astype(out.dtype)

    for c in pending:
        c.wait_send()
    if square:
        remote(token_block(1), token_block(1), tok_send.at[3], tok_recv.at[3], other).wait_send()

    @pl.when(a != b)
    def _():
        for s in range(h):
            remote(mine_h.at[s], mine_h.at[s], h_send.at[s, 0], h_recv.at[s, 0, 0], other).wait_send()


def local(G, n, B, tokens, gate_weight, up_weight, down_weight):
    h = n // B
    R, K = tokens.shape
    depth, wide = gate_weight.shape
    units, columns = wide // h, down_weight.shape[1]
    dtype = tokens.dtype
    DMA = pltpu.SemaphoreType.DMA
    return pl.pallas_call(
        functools.partial(layer, G, n, B),
        out_shape=jax.ShapeDtypeStruct((h * R, columns), dtype),
        in_specs=[ANY] * 4,
        out_specs=pl.BlockSpec(memory_space=pltpu.VMEM),
        scratch_shapes=[
            pltpu.VMEM((h, R, K), dtype),
            pltpu.VMEM((K, 2 * units), dtype),
            pltpu.VMEM((B, wide, columns), dtype),
            pltpu.VMEM((R, 2 * units), jnp.float32),
            pltpu.VMEM((h, R, units), dtype),
            pltpu.VMEM((h, h, B, R, units), dtype),
            pltpu.VMEM((h, R, columns), jnp.float32),
            DMA((4,)),
            DMA((h,)), DMA((h,)), DMA((h,)), DMA((h,)),
            DMA((n, 2)), DMA((n, 2)),
            DMA((G, n, 2)), DMA((G, n, 2)),
            DMA, DMA,
            DMA((h, n // 2)), DMA((h, h // 2, B)),
            DMA((h, h // 2, B)), DMA((h, h // 2, B)),
        ],
        compiler_params=pltpu.CompilerParams(
            collective_id=0, has_side_effects=True, vmem_limit_bytes=63_000_000
        ),
        name="layer",
    )(tokens, gate_weight, up_weight, down_weight)


def solution(mesh):
    shape = dict(mesh.shape)
    return jax.shard_map(
        functools.partial(local, shape["groups"], shape["tp"], shape["blk"]),
        mesh=mesh,
        in_specs=(P(("groups", "tp"), None), P("tp", "blk"), P("tp", "blk"), P("blk", "tp")),
        out_specs=P(("groups", "blk"), "tp"),
        check_vma=False,
    )
```

time: 531 us -> 207 us (0.39)
  waiting for transfers between devices: 474 us -> 0 us
  Pallas kernels: 0 us -> 203 us
  matrix products: 28.7 us -> 0 us
  between operations: 13.1 us -> 0.01 us
  starting transfers between devices: 5.96 us -> 0 us
    all_gather x4 -> x0, waiting for transfers between devices: 472 us -> none  [the longest x1 201 us: local(): lax.all_gather(gate_weight, 'tp', axis=0, tiled=True)]
    pallas_call x0 -> x1, Pallas kernels: none -> 203 us  [local(): pl.pallas_call(functools.partial(layer, G, n, B), out_shape=jax.ShapeDtyp...]
    dot_general x3 -> x0, matrix products: 28.7 us -> none  [the longest x1 11.1 us: local(): jnp.dot(tokens, lax.all_gather(up_weight, 'tp', axis=0, tiled=True), pref...]
    all_to_all x1 -> x0, local copies, waits for them, and re-layouts: 6.23 us -> none  [local(): lax.all_to_all(gathered, 'blk', split_axis=0, concat_axis=1, tiled=True)]
    all_to_all x1 -> x0, starting transfers between devices: 5.84 us -> none  [local(): lax.all_to_all(gathered, 'blk', split_axis=0, concat_axis=1, tiled=True)]
  transfers between devices with their start and end apart: 5 -> 0, of which waited for: 5 -> 0; matrix products, arithmetic and copies ran while one was open for 3% -> 0% of each run, Pallas kernels for 0% -> 0%
where the time goes in v2:
time: 207 us; the launch traced here: 206 us
  Pallas kernels  203 us (98%)
  local copies, waits for them, and re-layouts  2.87 us (1%)
    pallas_call x1, Pallas kernels, local(): pl.pallas_call(functools.partial(layer, G, n, B), out_shape=jax.ShapeDtyp...  203 us

profile of v2, /device:TPU:28, one launch (start us, length us, event | category | flops | bytes accessed | tf_op | source)
XLA Modules:
  0.0 206.2 jit_solution(15981131980132670351)
XLA Ops:
  0.0 203.4 %layer.1 = bf16[1024,896]{1,0:T(8,128)(2,1)} custom-call(bf16[256,7168]{1,0:T(8,128)(2,1)} %tok.1, bf16[896,1024]{1,0:T(8,128)(2,1)} %gate.1, bf16[896,1024]{1,0:T(8,128)(2,1)} %up.1, bf16[1024,896]{1,0:T(8,128)(2,1)} %down.1), custom_call_target="tpu_custom_call" | custom-call | tf_op jit(solution)/shard_map/layer/pallas_call | solution.py:238
  203.4 2.9 %copy.6 = bf16[1024,896]{1,0:T(8,128)(2,1)} copy(bf16[1024,896]{1,0:T(8,128)(2,1)} %layer.1) | data formatting | bytes 3670016

commit v3 on v2

--- a/solution.py
+++ b/solution.py
@@ -40,7 +40,7 @@
     half, pairs = h // 2, n // 2
     p, y = t // 2, t % 2
     other = (g, t, 1 - b)
-    across = (g, flip1(t), a * 0 + b)
+    across = (g, flip1(t), b)
     R, K = tok.shape
     width = K // B
     depth, units = gate.shape[0], gate.shape[1] // h
@@ -95,7 +95,7 @@
 
     first = g * part
     rows = pl.ds(pl.multiple_of(first, 16), part)
-    order = [n // 2] + [d for k in range(1, n // 2) for d in (n // 2 - k, n // 2 + k)]
+    order = [d for k in range(1, n // 2) for d in (k, n - k)] + [n // 2]
     for d in order:
         dest = (t + d) % n
         cols = pl.ds(pl.multiple_of((dest % h) * units, 128), units)

time: 207 us -> 188 us (0.908)
  Pallas kernels: 203 us -> 185 us
    pallas_call x1, Pallas kernels: 203 us -> 185 us  [local(): pl.pallas_call(functools.partial(layer, G, n, B), out_shape=jax.ShapeDtyp...]
where the time goes in v3:
time: 188 us
  Pallas kernels  185 us (98%)
  local copies, waits for them, and re-layouts  2.87 us (2%)
    pallas_call x1, Pallas kernels, local(): pl.pallas_call(functools.partial(layer, G, n, B), out_shape=jax.ShapeDtyp...  185 us

profile of v3, /device:TPU:28, one launch (start us, length us, event | category | flops | bytes accessed | tf_op | source)
XLA Modules:
  0.0 187.9 jit_solution(4931884393650530360)
XLA Ops:
  0.0 185.0 %layer.1 = bf16[1024,896]{1,0:T(8,128)(2,1)} custom-call(bf16[256,7168]{1,0:T(8,128)(2,1)} %tok.1, bf16[896,1024]{1,0:T(8,128)(2,1)} %gate.1, bf16[896,1024]{1,0:T(8,128)(2,1)} %up.1, bf16[1024,896]{1,0:T(8,128)(2,1)} %down.1), custom_call_target="tpu_custom_call" | custom-call | tf_op jit(solution)/shard_map/layer/pallas_call | solution.py:238
  185.0 2.9 %copy.6 = bf16[1024,896]{1,0:T(8,128)(2,1)} copy(bf16[1024,896]{1,0:T(8,128)(2,1)} %layer.1) | data formatting | bytes 3670016

commit v4 on v3

--- a/solution.py
+++ b/solution.py
@@ -24,6 +24,9 @@
 
 def flip2(i):
     return i + 2 - 4 * ((i // 2) % 2)
+
+
+CUT = 8
 
 
 def layer(
@@ -48,6 +51,8 @@
     mine = pl.ds(pl.multiple_of(b * width, 128), width)
     theirs = pl.ds(pl.multiple_of((1 - b) * width, 128), width)
     square = h == 4
+    cut = R * CUT // 16
+    upper, lower_rows = pl.ds(0, cut), pl.ds(cut, R - cut)
 
     greet(
         [(g, (t + d) % n, b) for d in range(1, n)]
@@ -126,12 +131,17 @@
 
     def tokens_arrive(s):
         block = token_block(s)
-        remote(block, block, tok_send.at[s], tok_recv.at[s], other).wait_recv()
+        if square and s == 3:
+            for i, r in ((3, upper), (0, lower_rows)):
+                piece = T.at[rows_of(j, s), r, mine]
+                remote(piece, piece, tok_send.at[i], tok_recv.at[i], other).wait_recv()
+        else:
+            remote(block, block, tok_send.at[s], tok_recv.at[s], other).wait_recv()
         if square and s < 3:
-            @pl.when(b == s - 1)
-            def _():
-                target = flip2(j) if s == 1 else flip1(j)
-                remote(block, block, tok_send.at[3], tok_recv.at[3], (g, a * h + target, b)).start()
+            piece = T.at[rows_of(j, s), (upper, lower_rows)[s - 1], mine]
+            target = flip2(j) if s == 1 else flip1(j)
+            i = 3 if s == 1 else 0
+            push(piece, piece, tok_send.at[i], tok_recv.at[i], (g, a * h + target, b))
 
         push(block, block, core_send.at[s], core_recv.at[s], other)
 
@@ -157,7 +167,7 @@
         def _():
             H[s, j, b] = hidden
 
-        for d in sorted(range(1, pairs), key=lambda d: -min(d, pairs - d)):
+        for d in sorted(range(1, pairs), key=lambda d: min(d, pairs - d)):
             push(
                 mine_h.at[s], H.at[s, j, b], h_send.at[s, d], h_recv.at[s, j // 2, b],
                 (g, 2 * ((p + d) % pairs) + y, a),
@@ -219,9 +229,6 @@
 
     for c in pending:
         c.wait_send()
-    if square:
-        remote(token_block(1), token_block(1), tok_send.at[3], tok_recv.at[3], other).wait_send()
-
     @pl.when(a != b)
     def _():
         for s in range(h):

time: 188 us -> 186 us (0.989)
  Pallas kernels: 185 us -> 182 us
    pallas_call x1, Pallas kernels: 185 us -> 182 us  [local(): pl.pallas_call(functools.partial(layer, G, n, B), out_shape=jax.ShapeDtyp...]
where the time goes in v4:
time: 186 us; the launch traced here: 185 us
  Pallas kernels  182 us (98%)
  local copies, waits for them, and re-layouts  2.87 us (2%)
    pallas_call x1, Pallas kernels, local(): pl.pallas_call(functools.partial(layer, G, n, B), out_shape=jax.ShapeDtyp...  182 us

profile of v4, /device:TPU:28, one launch (start us, length us, event | category | flops | bytes accessed | tf_op | source)
XLA Modules:
  0.0 185.2 jit_solution(7336265160710775946)
XLA Ops:
  0.0 182.3 %layer.1 = bf16[1024,896]{1,0:T(8,128)(2,1)} custom-call(bf16[256,7168]{1,0:T(8,128)(2,1)} %tok.1, bf16[896,1024]{1,0:T(8,128)(2,1)} %gate.1, bf16[896,1024]{1,0:T(8,128)(2,1)} %up.1, bf16[1024,896]{1,0:T(8,128)(2,1)} %down.1), custom_call_target="tpu_custom_call" | custom-call | tf_op jit(solution)/shard_map/layer/pallas_call | solution.py:245
  182.3 2.9 %copy.6 = bf16[1024,896]{1,0:T(8,128)(2,1)} copy(bf16[1024,896]{1,0:T(8,128)(2,1)} %layer.1) | data formatting | bytes 3670016
